TPU v7x, 256 devices: a 8x8x2 block of a 8x8x16 slice. The times are simulated.
256 devices in a mesh: groups: 2 (over z), cache: 16 (over x, core), tensor: 8 (over y).
Axes of the slice: x: 8, y: 8, z: 2, core: 2. Of those that a mesh axis runs over, the one named last changes fastest.
The devices are a block of a 8x8x16 slice.
Arguments:
- queries: bfloat16 [8192, 8192], P(('groups', 'cache'), 'tensor'), parts along dimension 0, may hold values from -8 to 8
- suffix_key_value: bfloat16 [2, 8192, 1024], P(None, ('groups', 'cache'), 'tensor'), parts along dimension 1, may hold values from -6 to 6
- kv_pages: bfloat16 [3072, 2, 128, 1024], P(('groups', 'cache'), None, None, 'tensor'), parts along dimension 0, may hold values from -6 to 6
- page_ids: int32 [32, 64], P(('groups', 'cache')), parts along dimension 0, may hold values from 0 to 1535, as said below
- prefix_pages: int32 [32], P(('groups', 'cache')), parts along dimension 0, may hold values from 8 to 64, as said below
- page_home: int32 [3072], P('groups'), parts along dimension 0, may hold values from 0 to 1535, as said below
- out_weight: bfloat16 [8192, 8192], P('tensor', 'cache'), may hold values from -0.25 to 0.25
Outputs:
- attended: bfloat16 [8192, 8192], P(('groups', 'cache'), 'tensor'), parts along dimension 0
There are 2 independent parts, one for each index of `groups`. A program takes and returns all parts, laid end to end along the dimension named above; an argument that names none is the same for every part. Nothing has to cross between parts.
Inputs may be any that keep to these rules, and one draw needn't show every extreme that they name: `page_ids`: live slots are j < prefix_pages[r]. Within the aligned block of 1 request of one index of cache, no page id appears twice among all 64 slots, and at most 6 of these slots name pages whose row page_home[id] lies on one index of cache (row // 96); in every such block some index of cache gets exactly 6. `prefix_pages`: one request in each draw has 64 pages and another has 8. `page_home`: A permutation of 0 to 1535.
All inputs are finite; a program needn't handle non-finite values.
Results may differ from a plain program's by a relative error of at most 0.015.
Values may be sent and summed in bfloat16 or wider, within the bound.
A program may use at most 128 MiB of HBM per device.

v0:
```python
import jax
import jax.numpy as jnp
from jax import lax
from jax.sharding import Mesh
from jax.sharding import PartitionSpec as P

QUERY_HEADS = 64
KEY_VALUE_HEADS = 8
HEAD_SIZE = 128
PAGE_TOKENS = 128
SUF = 256
MAXP = 64
CACHE = ("cache_0", "cache_1")
GROUPS_CACHE = ("groups", "cache_0", "cache_1")


masked_score = -1e30
pages_per_block = 4


def in_blocks(shard, dim, peers):
    lengths = shard.shape
    parts = shard.reshape(*lengths[:dim], peers, lengths[dim] // peers, *lengths[dim + 1 :])
    return jnp.moveaxis(parts, dim, 0)


def joined_along(parts, dim):
    lengths = list(parts.shape[1:])
    lengths[dim] *= parts.shape[0]
    return jnp.moveaxis(parts, 0, dim).reshape(lengths)


def moved_by_axis(parts, axes, order):
    inside = parts.shape[1:]
    whole = parts.reshape(*(lax.axis_size(a) for a in axes), *inside)
    for k in order:
        whole = lax.all_to_all(whole, axes[k], k, k, tiled=True)
    return whole.reshape(-1, *inside)


def stepwise_exchange(shard, axes, order, split_dim, concat_dim):
    parts = in_blocks(shard, split_dim, lax.axis_size(axes))
    return joined_along(moved_by_axis(parts, axes, order), concat_dim)


def on_gathered_pieces(shard, axis, dim, apply, out_dim):
    peers, width = (lax.axis_size(axis), shard.shape[dim])
    count = 2 if width % 2 == 0 else 1
    finished, length = ([], width // count)
    for k in range(count):
        piece = lax.slice_in_dim(shard, k * length, (k + 1) * length, axis=dim)
        starts = jnp.arange(peers) * width + k * length
        finished.append(jax.vmap(apply)(lax.all_gather(piece, axis), starts))
    return joined_along(jnp.concatenate(finished, axis=out_dim + 1), out_dim)


def per_device(queries, suffix_key_value, kv_pages, page_ids, prefix_pages, page_home, out_weight):
    cache_count = lax.axis_size(CACHE)
    request_count = page_ids.shape[0]
    capacity = (3 * request_count * MAXP + 2 * cache_count - 1) // (2 * cache_count)
    pool_rows = kv_pages.shape[0]
    kv_width = kv_pages.shape[3]
    kv_heads_here = kv_width // HEAD_SIZE
    group_width = QUERY_HEADS // KEY_VALUE_HEADS
    score_scale = HEAD_SIZE ** (-0.5)
    table_index = jnp.arange(page_home.shape[0], dtype=jnp.int32)
    owner_index = jnp.arange(cache_count, dtype=jnp.int32)
    buffer_index = jnp.arange(cache_count * capacity, dtype=jnp.int32)
    flat_ids = page_ids.reshape(-1)
    rows_of = jnp.sum(
        jnp.where(flat_ids[:, None] == table_index[None, :], page_home[None, :], 0), axis=1
    )
    owners = rows_of // pool_rows
    within = rows_of % pool_rows
    live_slots = (jnp.arange(MAXP, dtype=jnp.int32)[None, :] < prefix_pages[:, None]).reshape(-1)
    member = ((owners[:, None] == owner_index[None, :]) & live_slots[:, None]).astype(jnp.int32)
    earlier = jnp.cumsum(member, axis=0) - member
    rank_within = jnp.sum(earlier * member, axis=1)
    target = jnp.where(live_slots, owners * capacity + rank_within, -1)
    wanted = jnp.sum(
        jnp.where(target[:, None] == buffer_index[None, :], within[:, None], 0), axis=0
    )
    target, wanted = (target, wanted.reshape(cache_count, capacity))
    slot_ids = stepwise_exchange(wanted, CACHE, (1, 0), 0, 0)
    chosen = jnp.take(kv_pages, slot_ids.reshape(-1), axis=0)
    arrived = lax.all_to_all(
        chosen.reshape(slot_ids.shape + kv_pages.shape[1:]),
        CACHE,
        split_axis=0,
        concat_axis=0,
        tiled=True,
    )
    buffer = arrived.reshape(cache_count * capacity, 2, PAGE_TOKENS, kv_width)
    fetched = jnp.take(buffer, jnp.maximum(target, 0), axis=0).reshape(
        request_count, MAXP, 2, PAGE_TOKENS, kv_width
    )
    positions = jnp.arange(SUF, dtype=jnp.int32)
    causal = (positions[None, :] <= positions[:, None])[None, :, None, :]
    block_keys = pages_per_block * PAGE_TOKENS
    key_pages = jnp.arange(block_keys, dtype=jnp.int32) // PAGE_TOKENS
    query_block = queries.reshape(SUF, kv_heads_here, group_width, HEAD_SIZE)
    suffix_keys = suffix_key_value[0, 0:SUF].reshape(SUF, kv_heads_here, HEAD_SIZE)
    suffix_values = suffix_key_value[1, 0:SUF].reshape(SUF, kv_heads_here, HEAD_SIZE)
    scores = (
        jnp.einsum("skgd,tkd->ksgt", query_block, suffix_keys, preferred_element_type=jnp.float32)
        * score_scale
    )
    scores = jnp.where(causal, scores, masked_score)
    row_top = jnp.max(scores, axis=3)
    weights = jnp.where(causal, jnp.exp(scores - row_top[..., None]), 0.0)
    weight_sum = jnp.sum(weights, axis=3)
    accumulated = jnp.einsum(
        "ksgt,tkd->ksgd",
        weights.astype(jnp.bfloat16),
        suffix_values,
        preferred_element_type=jnp.float32,
    )
    pages_here = fetched[0]
    length = prefix_pages[0]
    block_count = (length + pages_per_block - 1) // pages_per_block

    def attend_block(block_index, state_now):
        top_now, sum_now, acc_now = state_now
        page_piece = lax.dynamic_slice_in_dim(
            pages_here, block_index * pages_per_block, pages_per_block, 0
        )
        key_rows = page_piece[:, 0].reshape(block_keys, kv_heads_here, HEAD_SIZE)
        value_rows = page_piece[:, 1].reshape(block_keys, kv_heads_here, HEAD_SIZE)
        live_keys = (block_index * pages_per_block + key_pages < length)[None, None, None, :]
        block_scores = (
            jnp.einsum("skgd,tkd->ksgt", query_block, key_rows, preferred_element_type=jnp.float32)
            * score_scale
        )
        block_scores = jnp.where(live_keys, block_scores, masked_score)
        new_top = jnp.maximum(top_now, jnp.max(block_scores, axis=3))
        factor = jnp.exp(top_now - new_top)
        block_weights = jnp.where(live_keys, jnp.exp(block_scores - new_top[..., None]), 0.0)
        new_sum = sum_now * factor + jnp.sum(block_weights, axis=3)
        new_acc = acc_now * factor[..., None] + jnp.einsum(
            "ksgt,tkd->ksgd",
            block_weights.astype(jnp.bfloat16),
            value_rows,
            preferred_element_type=jnp.float32,
        )
        return (new_top, new_sum, new_acc)

    row_top, weight_sum, accumulated = lax.fori_loop(
        0, block_count, attend_block, (row_top, weight_sum, accumulated)
    )
    mixed_heads = (accumulated / weight_sum[..., None]).astype(jnp.bfloat16)
    outputs = jnp.transpose(mixed_heads, (1, 0, 2, 3)).reshape(
        SUF, kv_heads_here * group_width * HEAD_SIZE
    )

    def project(weight_piece, start_column):
        return jnp.dot(outputs, weight_piece, preferred_element_type=jnp.float32)

    group_term = on_gathered_pieces(out_weight, CACHE, 1, project, 1)
    attended = lax.psum_scatter(
        group_term.astype(jnp.bfloat16), "tensor", scatter_dimension=1, tiled=True
    )
    return attended


def solution(mesh):
    split = Mesh(
        mesh.devices.reshape(mesh.shape["groups"], 8, 2, mesh.shape["tensor"]),
        ("groups", "cache_0", "cache_1", "tensor"),
    )
    placed = (
        P(GROUPS_CACHE, "tensor"),
        P(None, GROUPS_CACHE, "tensor"),
        P(GROUPS_CACHE, None, None, "tensor"),
        P(GROUPS_CACHE, None),
        P(GROUPS_CACHE),
        P("groups"),
        P("tensor", CACHE),
    )
    return jax.shard_map(
        per_device,
        mesh=split,
        in_specs=placed,
        out_specs=P(GROUPS_CACHE, "tensor"),
        check_vma=False,
    )
```

profile of v0, /device:TPU:521, one launch (start us, length us, event | category | flops | bytes accessed | tf_op | source)
XLA Modules:
  0.0 421.7 jit_solution(1721491830937339860)
XLA Ops:
  6.6 2.3 fusion.53
  9.5 0.9 select_reduce_fusion
  11.2 4.0 all_to_all.15
  15.2 22.8 %all_to_all.16 = s32[8,2,1,6]{3,1,2,0:T(2,128)S(1)} all-to-all(s32[8,2,1,6]{3,1,2,0:T(2,128)S(1)} %copy.42), channel_id=1, replica_groups=mesh['groups'=2,'cache_0'=8,'cache_1'=2,'tensor'=8] {'cache_0'}, dimensions={0} | all-to-all | bytes 768 | tf_op jit(solution)/shard_map/all_to_all | solution.py:37
  38.2 9.2 %gather_fusion = bf16[96,2,128,128]{3,2,1,0:T(8,128)(2,1)} fusion(bf16[96,2,128,128]{3,2,1,0:T(8,128)(2,1)} %param.11, s32[1024]{0:T(1024)S(1)} %pad_clamp_fusion.1), kind=kCustom, calls=%fused_computation | custom fusion | bytes 12583296 | tf_op jit(solution)/shard_map/jit(_take)/gather | solution.py:85
  47.4 6.2 %broadcast_select_fusion = bf16[16,6,2,128,128]{4,3,2,1,0:T(8,128)(2,1)} fusion(bf16[16,6,2,128,128]{4,3,2,1,0:T(8,128)(2,1)} %bitcast.142, pred[16,6]{1,0:T(8,128)(4,1)S(1)} %compare_and_fusion), kind=kLoop, calls=%fused_computation.35 | loop fusion | flops 3145728 | bytes 12583008 | tf_op jit(solution)/shard_map/jit(_take)/select_n | solution.py:85
  53.6 10.6 %all-to-all-start.2 = ((bf16[16,6,2,128,128]{4,3,2,1,0:T(8,128)(2,1)}), bf16[16,6,2,128,128]{4,3,2,1,0:T(8,128)(2,1)}, u32[]{:S(2)}, u32[]{:S(2)}) async-start(bf16[16,6,2,128,128]{4,3,2,1,0:T(8,128)(2,1)} %broadcast_select_fusion), calls=%async_computation.2 | async-start | bytes 12582912 | tf_op jit(solution)/shard_map/all_to_all | solution.py:86
  67.6 164.1 %all-to-all-done.2 = bf16[16,6,2,128,128]{4,3,2,1,0:T(8,128)(2,1)} async-done(((bf16[16,6,2,128,128]{4,3,2,1,0:T(8,128)(2,1)}), bf16[16,6,2,128,128]{4,3,2,1,0:T(8,128)(2,1)}, u32[]{:S(2)}, u32[]{:S(2)}) %all-to-all-start.2) | async-done | bytes 6291488 | tf_op jit(solution)/shard_map/all_to_all | solution.py:86
  231.7 6.1 %gather_fusion.1 = bf16[64,2,128,128]{3,2,1,0:T(8,128)(2,1)} fusion(bf16[96,2,128,128]{3,2,1,0:T(8,128)(2,1)} %bitcast.12, s32[1024]{0:T(1024)S(1)} %pad_clamp_fusion), kind=kCustom, calls=%fused_computation.1 | custom fusion | bytes 8388864 | tf_op jit(solution)/shard_map/jit(_take)/gather | solution.py:94
  237.8 4.7 %broadcast_select_fusion.1 = bf16[64,2,128,128]{3,2,1,0:T(8,128)(2,1)} fusion(bf16[64,2,128,128]{3,2,1,0:T(8,128)(2,1)} %gather_fusion.1, pred[64]{0:T(512)(128)(4,1)S(1)} %get-tuple-element.117), kind=kLoop, calls=%fused_computation.37 | loop fusion | flops 2097152 | bytes 8388672 | tf_op jit(solution)/shard_map/jit(_take)/select_n | solution.py:94
  242.5 92.3 %while.15 = (s32[]{:T(128)}, f32[1,256,8]{1,2,0:T(8,128)S(1)}, f32[1,256,8]{1,2,0:T(8,128)S(1)}, f32[1,256,8,128]{3,1,2,0:T(8,128)S(1)}, s32[]{:T(128)}, /*index...) while((s32[]{:T(128)}, f32[1,256,8]{1,2,0:T(8,128)S(1)}, ...), condition=%wide.region_9.10_spmd.clone, body=%wide.region_6.9_spmd.clone.sunk | while | flops 551037952 | bytes 16124103 | solution.py:147
  242.5 1.0 constant_dynamic-slice_fusion.3
  245.0 2.1 fusion.74
  247.1 1.2 fusion.73
  248.3 1.0 constant_dynamic-slice_fusion.3
  250.7 2.1 fusion.74
  252.8 1.2 fusion.73
  254.0 1.0 constant_dynamic-slice_fusion.3
  256.5 2.1 fusion.74
  258.6 1.2 fusion.73
  259.8 1.0 constant_dynamic-slice_fusion.3
  262.3 2.1 fusion.74
  264.4 1.2 fusion.73
  265.6 1.0 constant_dynamic-slice_fusion.3
  268.0 2.1 fusion.74
  270.1 1.2 fusion.73
  271.3 1.0 constant_dynamic-slice_fusion.3
  273.8 2.1 fusion.74
  275.9 1.2 fusion.73
  277.1 1.0 constant_dynamic-slice_fusion.3
  279.5 2.1 fusion.74
  281.6 1.2 fusion.73
  282.8 1.0 constant_dynamic-slice_fusion.3
  285.3 2.1 fusion.74
  287.4 1.2 fusion.73
  288.6 1.0 constant_dynamic-slice_fusion.3
  291.0 2.1 fusion.74
  293.1 1.2 fusion.73
  294.4 1.0 constant_dynamic-slice_fusion.3
  296.8 2.1 fusion.74
  298.9 1.2 fusion.73
  300.1 1.0 constant_dynamic-slice_fusion.3
  302.6 2.1 fusion.74
  304.7 1.2 fusion.73
  305.9 1.0 constant_dynamic-slice_fusion.3
  308.3 2.1 fusion.74
  310.4 1.2 fusion.73
  311.6 1.0 constant_dynamic-slice_fusion.3
  314.1 2.1 fusion.74
  316.2 1.2 fusion.73
  317.4 1.0 constant_dynamic-slice_fusion.3
  319.8 2.1 fusion.74
  321.9 1.2 fusion.73
  323.1 1.0 constant_dynamic-slice_fusion.3
  325.6 2.1 fusion.74
  327.7 1.2 fusion.73
  328.9 1.0 constant_dynamic-slice_fusion.3
  331.3 2.1 fusion.74
  333.4 1.2 fusion.73
  335.3 6.8 %convert_bitcast_fusion = bf16[16,256,256]{1,2,0:T(8,128)(2,1)S(1)} fusion(bf16[256,1024,1]{0,1,2:T(8,128)(2,1)S(1)} %bitcast.150, bf16[16,1024,256]{2,1,0:T(8,128)(2,1)} %bitcast.156), kind=kOutput, calls=%fused_computation.38 | convolution fusion | flops 2148532224 | bytes 11010048 | tf_op jit(solution)/shard_map/vmap()/dot_general | solution.py:156
  342.2 6.8 %convert_bitcast_fusion.1 = bf16[16,256,256]{1,2,0:T(8,128)(2,1)S(1)} fusion(bf16[256,1024,1]{0,1,2:T(8,128)(2,1)S(1)} %bitcast.151, bf16[16,1024,256]{2,1,0:T(8,128)(2,1)} %bitcast.157), kind=kOutput, calls=%fused_computation.39 | convolution fusion | flops 2148532224 | bytes 11010048 | tf_op jit(solution)/shard_map/vmap()/dot_general | solution.py:156
  349.0 2.3 pad_maximum_fusion
  351.3 6.4 %copy.51 = bf16[256,8192]{1,0:T(8,128)(2,1)} copy(bf16[256,8192]{0,1:T(8,128)(2,1)} %bitcast.143) | data formatting | bytes 8388608 | tf_op jit(solution)/shard_map/convert_element_type | solution.py:160
  357.7 57.5 %reduce-scatter.2.cloned.1.call-done = bf16[256,1024]{1,0:T(8,128)(2,1)} async-done(((bf16[256,8192]{1,0:T(8,128)(2,1)}), bf16[256,1024]{1,0:T(8,128)(2,1)}) %reduce-scatter.2.cloned.1.call-update) | async-done | bytes 524304 | tf_op jit(solution)/shard_map/reduce_scatter | solution.py:159
  (116 shorter events, 27.6 us)
Async XLA Ops:
  6.5 328.8 %all-gather.7.cloned.1.call-start = ((), (), s32[]{:S(2)}) async-start(), calls=%async_computation.6 | async-start | bytes 8912896 | tf_op jit(solution)/shard_map/all_gather | solution.py:53
  53.6 11.5 %copy-start = (bf16[256,1024]{1,0:T(8,128)(2,1)S(1)}, bf16[256,1024]{1,0:T(8,128)(2,1)}, u32[]{:S(2)}) copy-start(bf16[256,1024]{1,0:T(8,128)(2,1)} %param.9) | copy-start | bytes 1572868
  53.6 12.1 %copy-start.1 = (bf16[2,256,128]{2,1,0:T(8,128)(2,1)S(1)}, bf16[2,256,128]{2,1,0:T(8,128)(2,1)}, u32[]{:S(2)}) copy-start(bf16[2,256,128]{2,1,0:T(8,128)(2,1)} %param.10) | copy-start | bytes 393220
  53.6 178.1 %all-to-all-start.2 = ((bf16[16,6,2,128,128]{4,3,2,1,0:T(8,128)(2,1)}), bf16[16,6,2,128,128]{4,3,2,1,0:T(8,128)(2,1)}, u32[]{:S(2)}, u32[]{:S(2)}) async-start(bf16[16,6,2,128,128]{4,3,2,1,0:T(8,128)(2,1)} %broadcast_select_fusion), calls=%async_computation.2 | async-start | bytes 12582912 | tf_op jit(solution)/shard_map/all_to_all | solution.py:86
  64.2 277.9 %all-gather.5.cloned.1.call-start = ((), (), s32[]{:S(2)}) async-start(), calls=%async_computation.5 | async-start | bytes 8912896 | tf_op jit(solution)/shard_map/all_gather | solution.py:53
  65.1 350.1 %reduce-scatter.2.cloned.1.call-start = ((), (), s32[]{:S(2)}) async-start(), calls=%async_computation.4 | async-start | bytes 4718592 | tf_op jit(solution)/shard_map/reduce_scatter | solution.py:159
Sparse Core Ops, SparseCore 0:
  9.2 117.0 all-gather.6
  128.2 127.4 all-gather.4
  357.8 57.3 reduce-scatter.1
where the time goes:
time: 425 us; the launch traced here: 422 us
  waiting for transfers between devices  222 us (52%)
  matrix products  60.7 us (14%)
  other arithmetic  44.6 us (10%)
  local copies, waits for them, and re-layouts  41.1 us (10%)
  blocking collectives  26.8 us (6%)
  between operations  14 us (3%)
  starting transfers between devices  10.8 us (3%)
    all_to_all x1, waiting for transfers between devices, per_device(): lax.all_to_all(chosen.reshape(slot_ids.shape + kv_pages.shape[1:]), CACHE...  164 us
    reduce_scatter x1, waiting for transfers between devices, per_device(): lax.psum_scatter(group_term.astype(jnp.bfloat16), 'tensor', scatter_dimen...  57.5 us
    dot_general x16, matrix products, attend_block(): jnp.einsum('ksgt,tkd->ksgd', block_weights.astype(jnp.bfloat16), value_ro...  33.6 us
    all_to_all x2, blocking collectives, moved_by_axis(): whole = lax.all_to_all(whole, axes[k], k, k, tiled=True)  26.8 us
    reduce_sum x16, other arithmetic, attend_block(): new_sum = sum_now * factor + jnp.sum(block_weights, axis=3)  18.5 us
    slice x16, local copies, waits for them, and re-layouts, attend_block(): value_rows = page_piece[:, 1].reshape(block_keys, kv_heads_here, HEAD_SIZE)  16 us
    dot_general x2, matrix products, project(): return jnp.dot(outputs, weight_piece, preferred_element_type=jnp.float32)  13.7 us
    dot_general x16, matrix products, attend_block(): jnp.einsum('skgd,tkd->ksgt', query_block, key_rows, preferred_element_typ...  12 us
  transfers between devices with their start and end apart: 4, of which 2 were waited for; matrix products, arithmetic and copies ran while one was open for 30% of the time, Pallas kernels for 0%

commit v1 on v0

v1 whole, which is shorter than its diff:
```python
import functools

import jax
import jax.numpy as jnp
from jax import lax
from jax.experimental import pallas as pl
from jax.experimental.pallas import tpu as pltpu
from jax.sharding import Mesh
from jax.sharding import PartitionSpec as P

QUERY_HEADS = 64
KEY_VALUE_HEADS = 8
HEAD_SIZE = 128
PAGE_TOKENS = 128
SUF = 256
MAXP = 64
CACHE = ("cache_0", "cache_1")
GROUPS_CACHE = ("groups", "cache_0", "cache_1")
GROUP_WIDTH = QUERY_HEADS // KEY_VALUE_HEADS

LOG2_SCALE = HEAD_SIZE ** (-0.5) * 1.4426950408889634
DEAD = 1e30
HALF = SUF // 2
OUT_ROWS = GROUP_WIDTH * HEAD_SIZE
PART_ROWS = OUT_ROWS + 32
VALUE_ROWS = HEAD_SIZE + 16
MESH = pl.DeviceIdType.MESH


def joined_along(parts, dim):
    lengths = list(parts.shape[1:])
    lengths[dim] *= parts.shape[0]
    return jnp.moveaxis(parts, 0, dim).reshape(lengths)


def on_gathered_pieces(shard, axis, dim, apply, out_dim):
    peers, width = (lax.axis_size(axis), shard.shape[dim])
    count = 2 if width % 2 == 0 else 1
    finished, length = ([], width // count)
    for k in range(count):
        piece = lax.slice_in_dim(shard, k * length, (k + 1) * length, axis=dim)
        starts = jnp.arange(peers) * width + k * length
        finished.append(jax.vmap(apply)(lax.all_gather(piece, axis), starts))
    return joined_along(jnp.concatenate(finished, axis=out_dim + 1), out_dim)


def attention_kernel(
    capacity,
    chips,
    table,
    live,
    q_hbm,
    kv_hbm,
    suffix_hbm,
    out,
    pool,
    suffix,
    q_all,
    part,
    partner_part,
    ring_in,
    keys,
    values_t,
    scores,
    weights,
    tops,
    sums,
    local_sem,
    q_send,
    q_recv,
    q_core_send,
    q_core_recv,
    p_core_send,
    p_core_recv,
    p_send,
    p_recv,
):
    x = lax.axis_index("cache_0")
    core = lax.axis_index("cache_1")
    right = {"cache_0": lax.rem(x + 1, chips), "cache_1": core}
    left = {"cache_0": lax.rem(x + chips - 1, chips), "cache_1": core}
    partner = {"cache_0": x, "cache_1": 1 - core}
    far = chips // 2
    toward = (right, left)

    fetch_q = pltpu.make_async_copy(q_hbm, q_all.at[0, 0], local_sem.at[0])
    fetch_pool = pltpu.make_async_copy(kv_hbm, pool, local_sem.at[1])
    fetch_suffix = pltpu.make_async_copy(suffix_hbm, suffix, local_sem.at[2])
    fetch_q.start()
    fetch_pool.start()
    fetch_suffix.start()
    barrier = pltpu.get_barrier_semaphore()
    for peer in (right, left, partner):
        pl.semaphore_signal(barrier, inc=1, device_id=peer, device_id_type=MESH)
    values_t[HEAD_SIZE:, :] = jnp.ones((VALUE_ROWS - HEAD_SIZE, values_t.shape[1]), jnp.bfloat16)
    fetch_q.wait()
    pl.semaphore_wait(barrier, 3)

    def chunk(offset, kind, half):
        return q_all.at[offset % chips, kind, pl.ds(half * HALF, HALF), :]

    def q_copy(direction, step, half):
        sign = -1 if direction == 0 else 1
        return pltpu.make_async_remote_copy(
            src_ref=chunk(sign * (step - 1), 0, half),
            dst_ref=chunk(sign * step, 0, half),
            send_sem=q_send.at[direction, step - 1, half],
            recv_sem=q_recv.at[direction, step - 1, half],
            device_id=toward[direction],
            device_id_type=MESH,
        )

    def q_core_copy(offset, half):
        return pltpu.make_async_remote_copy(
            src_ref=chunk(offset, 0, half),
            dst_ref=chunk(offset, 1, half),
            send_sem=q_core_send.at[offset % chips, half],
            recv_sem=q_core_recv.at[offset % chips, half],
            device_id=partner,
            device_id_type=MESH,
        )

    def p_core_copy(offset):
        return pltpu.make_async_remote_copy(
            src_ref=part.at[offset % chips, 1],
            dst_ref=partner_part.at[offset % chips],
            send_sem=p_core_send.at[offset % chips],
            recv_sem=p_core_recv.at[offset % chips],
            device_id=partner,
            device_id_type=MESH,
        )

    def p_copy(direction, distance, half):
        sign = 1 if direction == 0 else -1
        return pltpu.make_async_remote_copy(
            src_ref=part.at[(sign * distance) % chips, 0, half],
            dst_ref=ring_in.at[direction, distance - 1, half],
            send_sem=p_send.at[direction, distance - 1, half],
            recv_sem=p_recv.at[direction, distance - 1, half],
            device_id=toward[direction],
            device_id_type=MESH,
        )

    def attend(offset, kind, own):
        where = offset % chips
        request = 2 * lax.rem(x + where, chips) + (core if kind == 0 else 1 - core)
        pages = capacity + (SUF // PAGE_TOKENS if own else 0)
        alive = []
        for j in range(capacity):
            row = table[request, j]
            alive.append(live[request, j])
            keys[j * PAGE_TOKENS : (j + 1) * PAGE_TOKENS, :] = pool[row, 0]
            values_t[0:HEAD_SIZE, j * PAGE_TOKENS : (j + 1) * PAGE_TOKENS] = pool[row, 1].T
        if own:
            keys[capacity * PAGE_TOKENS :, :] = suffix[0]
            values_t[0:HEAD_SIZE, capacity * PAGE_TOKENS :] = suffix[1].T

        def head(h, carry):
            q_head = q_all[where, kind, :, pl.ds(pl.multiple_of(h * HEAD_SIZE, HEAD_SIZE), HEAD_SIZE)]
            top = None
            for j in range(pages):
                span = pl.ds(j * PAGE_TOKENS, PAGE_TOKENS)
                piece = lax.dot_general(
                    keys[span, :], q_head, (((1,), (1,)), ((), ())), preferred_element_type=jnp.float32
                )
                if j >= capacity:
                    key_at = lax.broadcasted_iota(jnp.int32, piece.shape, 0) + (j - capacity) * PAGE_TOKENS
                    token_at = lax.broadcasted_iota(jnp.int32, piece.shape, 1)
                    piece = jnp.where(key_at <= token_at, piece, -DEAD)
                scores[span, :] = piece
                peak = jnp.max(piece, axis=0, keepdims=True)
                if j < capacity:
                    peak = peak * alive[j] + (alive[j] - 1.0) * DEAD
                top = peak if top is None else jnp.maximum(top, peak)
            level = jnp.ceil(top * (LOG2_SCALE * 0.25)) * 4.0
            for j in range(pages):
                span = pl.ds(j * PAGE_TOKENS, PAGE_TOKENS)
                shift = -level
                if j < capacity:
                    shift = shift * alive[j] + (alive[j] - 1.0) * DEAD
                weights[span, :] = jnp.exp2(scores[span, :] * LOG2_SCALE + shift).astype(jnp.bfloat16)
            length = pages * PAGE_TOKENS
            mixed = jnp.dot(values_t[:, 0:length], weights[0:length, :], preferred_element_type=jnp.float32)
            rows = pl.ds(pl.multiple_of(h * HEAD_SIZE, HEAD_SIZE), HEAD_SIZE)
            low = mixed[0:HEAD_SIZE].astype(jnp.bfloat16)
            part[where, kind, 0, rows, :] = low[:, 0:HALF]
            part[where, kind, 1, rows, :] = low[:, HALF:]
            tops[pl.ds(h, 1), :] = level
            sums[pl.ds(h, 1), :] = mixed[HEAD_SIZE : HEAD_SIZE + 1]
            return carry

        lax.fori_loop(0, GROUP_WIDTH, head, 0)
        for half in range(2):
            lanes = pl.ds(half * HALF, HALF)
            put_stats(part.at[where, kind, half], tops[:, lanes], sums[:, lanes])

    def put_stats(ref, top, total):
        high = total.astype(jnp.bfloat16).astype(jnp.float32)
        stats = jnp.concatenate([top, high, total - high, jnp.zeros_like(top)], axis=0)
        ref[OUT_ROWS:PART_ROWS, :] = stats.astype(jnp.bfloat16)

    def get_stats(ref):
        stats = ref[OUT_ROWS:PART_ROWS, :].astype(jnp.float32)
        return stats[0:8], stats[8:16] + stats[16:24]

    def merge(ref, others):
        pairs = [get_stats(r) for r in [ref] + others]
        top = functools.reduce(jnp.maximum, [p[0] for p in pairs])
        factors = [jnp.exp2(p[0] - top) for p in pairs]
        total = sum(p[1] * f for p, f in zip(pairs, factors))
        for h in range(GROUP_WIDTH):
            rows = slice(h * HEAD_SIZE, (h + 1) * HEAD_SIZE)
            acc = sum(
                r[rows, :].astype(jnp.float32) * f[h : h + 1]
                for r, f in zip([ref] + others, factors)
            )
            ref[rows, :] = acc.astype(jnp.bfloat16)
        put_stats(ref, top, total)

    halves = (0, 1)
    for half in halves:
        for direction in (0, 1):
            q_copy(direction, 1, half).start()
        q_core_copy(0, half).start()
    fetch_pool.wait()
    fetch_suffix.wait()
    attend(0, 0, True)
    pending = []

    def arrived(step, direction, half):
        q_copy(direction, step, half).wait_recv()
        if step + 1 < far or (step + 1 == far and half == direction):
            q_copy(direction, step + 1, half).start()
        q_core_copy(-step if direction == 0 else step, half).start()

    def other_core(offset):
        for half in halves:
            q_core_copy(offset, half).wait_recv()
        attend(offset, 1, False)
        p_core_copy(offset).start()

    for step in range(1, far):
        for direction in (0, 1):
            arrived(step, direction, 0)
        if step == 1:
            other_core(0)
        else:
            other_core(1 - step)
            other_core(step - 1)
        for direction in (0, 1):
            arrived(step, direction, 1)
        attend(-step, 0, False)
        attend(step, 0, False)
    arrived(far, 0, 0)
    arrived(far, 1, 1)
    attend(far, 0, False)
    other_core(far)
    other_core(1 - far)
    other_core(far - 1)

    p_core_copy(far).wait_recv()
    for direction in (0, 1):
        half = direction
        merge(part.at[far, 0, half], [partner_part.at[far, half]])
        p_copy(direction, far, half).start()
    for distance in range(far - 1, 0, -1):
        for direction in (0, 1):
            offset = (distance if direction == 0 else -distance) % chips
            p_core_copy(offset).wait_recv()
        for turn in (0, 1):
            for direction in (0, 1):
                offset = (distance if direction == 0 else -distance) % chips
                half = direction if turn == 1 else 1 - direction
                others = [partner_part.at[offset, half]]
                if distance < far - 1 or half == direction:
                    p_copy(direction, distance + 1, half).wait_recv()
                    others.append(ring_in.at[direction, distance, half])
                merge(part.at[offset, 0, half], others)
                p_copy(direction, distance, half).start()
    p_core_copy(0).wait_recv()
    for half in halves:
        for direction in (0, 1):
            p_copy(direction, 1, half).wait_recv()
        refs = [part.at[0, 0, half], partner_part.at[0, half], ring_in.at[0, 0, half], ring_in.at[1, 0, half]]
        pairs = [get_stats(r) for r in refs]
        top = functools.reduce(jnp.maximum, [p[0] for p in pairs])
        factors = [jnp.exp2(p[0] - top) for p in pairs]
        total = sum(p[1] * f for p, f in zip(pairs, factors))
        factors = [f / total for f in factors]
        for h in range(GROUP_WIDTH):
            rows = slice(h * HEAD_SIZE, (h + 1) * HEAD_SIZE)
            acc = sum(r[rows, :].astype(jnp.float32) * f[h : h + 1] for r, f in zip(refs, factors))
            out[half * HALF : (half + 1) * HALF, rows] = acc.T.astype(jnp.bfloat16)

    for direction in (0, 1):
        for half in halves:
            for step in range(1, far + 1):
                if step < far or half == direction:
                    q_copy(direction, step, half).wait_send()
                    p_copy(direction, step, half).wait_send()
    for offset in range(chips):
        for half in halves:
            q_core_copy(offset, half).wait_send()
        p_core_copy(offset).wait_send()


def attention(table, live, queries, kv_pages, suffix_key_value):
    chips = lax.axis_size("cache_0")
    capacity = table.shape[1]
    far = chips // 2
    long = capacity * PAGE_TOKENS + SUF
    bf16 = jnp.bfloat16
    requests = table.shape[0]
    any_space = pl.BlockSpec(memory_space=pl.ANY)
    flops = 4 * requests * GROUP_WIDTH * SUF * HEAD_SIZE * capacity * PAGE_TOKENS
    dma = pltpu.SemaphoreType.DMA
    return pl.pallas_call(
        functools.partial(attention_kernel, capacity, chips),
        out_shape=jax.ShapeDtypeStruct(queries.shape, bf16),
        in_specs=[
            pl.BlockSpec(memory_space=pltpu.SMEM),
            pl.BlockSpec(memory_space=pltpu.SMEM),
            any_space,
            any_space,
            any_space,
        ],
        out_specs=pl.BlockSpec(memory_space=pltpu.VMEM),
        scratch_shapes=[
            pltpu.VMEM(kv_pages.shape, bf16),
            pltpu.VMEM(suffix_key_value.shape, bf16),
            pltpu.VMEM((chips, 2) + queries.shape, bf16),
            pltpu.VMEM((chips, 2, 2, PART_ROWS, HALF), bf16),
            pltpu.VMEM((chips, 2, PART_ROWS, HALF), bf16),
            pltpu.VMEM((2, far, 2, PART_ROWS, HALF), bf16),
            pltpu.VMEM((long, HEAD_SIZE), bf16),
            pltpu.VMEM((VALUE_ROWS, long), bf16),
            pltpu.VMEM((long, SUF), jnp.float32),
            pltpu.VMEM((long, SUF), bf16),
            pltpu.VMEM((GROUP_WIDTH, SUF), jnp.float32),
            pltpu.VMEM((GROUP_WIDTH, SUF), jnp.float32),
            dma((3,)),
            dma((2, far, 2)),
            dma((2, far, 2)),
            dma((chips, 2)),
            dma((chips, 2)),
            dma((chips,)),
            dma((chips,)),
            dma((2, far, 2)),
            dma((2, far, 2)),
        ],
        compiler_params=pltpu.CompilerParams(
            collective_id=0, has_side_effects=True, vmem_limit_bytes=60 * 1024 * 1024
        ),
        cost_estimate=pl.CostEstimate(
            flops=8 * flops, bytes_accessed=kv_pages.size * 2, transcendentals=0
        ),
        name="ring_attention",
    )(table, live, queries, kv_pages, suffix_key_value)


def slot_tables(kv_pages, page_ids, prefix_pages, page_home):
    cache_count = lax.axis_size(CACHE)
    request_count = page_ids.shape[0]
    capacity = (3 * request_count * MAXP + 2 * cache_count - 1) // (2 * cache_count)
    pool_rows = kv_pages.shape[0]
    table_index = jnp.arange(page_home.shape[0], dtype=jnp.int32)
    owner_index = jnp.arange(cache_count, dtype=jnp.int32)
    buffer_index = jnp.arange(cache_count * capacity, dtype=jnp.int32)
    flat_ids = page_ids.reshape(-1)
    rows_of = jnp.sum(
        jnp.where(flat_ids[:, None] == table_index[None, :], page_home[None, :], 0), axis=1
    )
    owners = rows_of // pool_rows
    within = rows_of % pool_rows
    live_slots = (jnp.arange(MAXP, dtype=jnp.int32)[None, :] < prefix_pages[:, None]).reshape(-1)
    member = ((owners[:, None] == owner_index[None, :]) & live_slots[:, None]).astype(jnp.int32)
    earlier = jnp.cumsum(member, axis=0) - member
    rank_within = jnp.sum(earlier * member, axis=1)
    target = jnp.where(live_slots, owners * capacity + rank_within, -1)
    wanted = jnp.sum(
        jnp.where(target[:, None] == buffer_index[None, :], within[:, None] + 1, 0), axis=0
    )
    everyone = lax.all_gather(wanted, CACHE).reshape(cache_count, cache_count, capacity)
    mine = lax.dynamic_index_in_dim(everyone, lax.axis_index(CACHE), 1, keepdims=False)
    return jnp.maximum(mine - 1, 0), (mine > 0).astype(jnp.float32)


def per_device(queries, suffix_key_value, kv_pages, page_ids, prefix_pages, page_home, out_weight):
    table, live = slot_tables(kv_pages, page_ids, prefix_pages, page_home)
    outputs = attention(table, live, queries, kv_pages, suffix_key_value)

    def project(weight_piece, start_column):
        return jnp.dot(outputs, weight_piece, preferred_element_type=jnp.float32)

    group_term = on_gathered_pieces(out_weight, CACHE, 1, project, 1)
    attended = lax.psum_scatter(
        group_term.astype(jnp.bfloat16), "tensor", scatter_dimension=1, tiled=True
    )
    return attended


def solution(mesh):
    cores = 2
    chips = mesh.shape["cache"] // cores
    split = Mesh(
        mesh.devices.reshape(mesh.shape["groups"], chips, cores, mesh.shape["tensor"]),
        ("groups", "cache_0", "cache_1", "tensor"),
    )
    placed = (
        P(GROUPS_CACHE, "tensor"),
        P(None, GROUPS_CACHE, "tensor"),
        P(GROUPS_CACHE, None, None, "tensor"),
        P(GROUPS_CACHE, None),
        P(GROUPS_CACHE),
        P("groups"),
        P("tensor", CACHE),
    )
    return jax.shard_map(
        per_device,
        mesh=split,
        in_specs=placed,
        out_specs=P(GROUPS_CACHE, "tensor"),
        check_vma=False,
    )
```

time: 425 us -> 305 us (0.72)
  waiting for transfers between devices: 222 us -> 66.5 us
  Pallas kernels: 0 us -> 135 us
  matrix products: 60.7 us -> 13.9 us
  other arithmetic: 44.6 us -> 3.68 us
  blocking collectives: 26.8 us -> 57 us
  local copies, waits for them, and re-layouts: 41.1 us -> 11.9 us
  starting transfers between devices: 10.8 us -> 0.13 us
    all_to_all x1 -> x0, waiting for transfers between devices: 164 us -> none  [per_device(): lax.all_to_all(chosen.reshape(slot_ids.shape + kv_pages.shape[1:]), CACHE...]
    pallas_call x0 -> x1, Pallas kernels: none -> 135 us  [attention(): pl.pallas_call(functools.partial(attention_kernel, capacity, chips), out_...]
    unnamed x0 -> x1, blocking collectives: none -> 57 us
    dot_general x34 -> x0, matrix products: 47 us -> none  [the longest x16 33.6 us: attend_block(): jnp.einsum('ksgt,tkd->ksgd', block_weights.astype(jnp.bfloat16), value_ro...]
    all_to_all x2 -> x0, blocking collectives: 26.8 us -> none  [moved_by_axis(): whole = lax.all_to_all(whole, axes[k], k, k, tiled=True)]
    reduce_sum x20 -> x3, other arithmetic: 20.2 us -> 1.19 us  [the longest x1 0.91 us: slot_tables(): jnp.sum(jnp.where(flat_ids[:, None] == table_index[None, :], page_home[No...]
    slice x16 -> x0, local copies, waits for them, and re-layouts: 16 us -> none  [attend_block(): value_rows = page_piece[:, 1].reshape(block_keys, kv_heads_here, HEAD_SIZE)]
    gather x2 -> x0, local copies, waits for them, and re-layouts: 15.3 us -> none  [the longest x1 9.2 us: per_device(): chosen = jnp.take(kv_pages, slot_ids.reshape(-1), axis=0)]
  transfers between devices with their start and end apart: 4 -> 3, of which waited for: 2 -> 1; matrix products, arithmetic and copies ran while one was open for 30% -> 4% of each run, Pallas kernels for 0% -> 45%
where the time goes in v1:
time: 305 us; the launch traced here: 303 us
  Pallas kernels  135 us (44%)
  waiting for transfers between devices  66.5 us (22%)
  blocking collectives  57 us (19%)
  between operations  14.6 us (5%)
  matrix products  13.9 us (5%)
  local copies, waits for them, and re-layouts  11.9 us (4%)
  other arithmetic  3.68 us (1%)
    pallas_call x1, Pallas kernels, attention(): pl.pallas_call(functools.partial(attention_kernel, capacity, chips), out_...  135 us
    reduce_scatter x1, waiting for transfers between devices, per_device(): lax.psum_scatter(group_term.astype(jnp.bfloat16), 'tensor', scatter_dimen...  65.6 us
    unnamed x1, blocking collectives  57 us
    dot_general x2, matrix products, project(): return jnp.dot(outputs, weight_piece, preferred_element_type=jnp.float32)  13.9 us
    convert_element_type x1, local copies, waits for them, and re-layouts, per_device(): group_term.astype(jnp.bfloat16)  6.38 us
  transfers between devices with their start and end apart: 3, of which 1 were waited for; matrix products, arithmetic and copies ran while one was open for 4% of the time, Pallas kernels for 45%

profile of v1, /device:TPU:521, one launch (start us, length us, event | category | flops | bytes accessed | tf_op | source)
XLA Modules:
  0.0 303.0 jit_solution(15850977264493372114)
XLA Ops:
  6.5 0.0 all-gather.6.cloned.1.call-start
  6.6 2.2 fusion.5
  8.8 0.1 all-gather.6.cloned.1.call-update
  8.8 0.1 all-gather.8.cloned.1.call-start
  8.9 0.7 all-gather.8.cloned.1.call-update
  9.7 0.1 reduce-scatter.2.cloned.1.call-start
  10.4 0.9 select_reduce_fusion
  11.3 0.1 fusion.3
  11.4 0.1 reduce_window_sum.11
  11.5 1.3 dynamic-slice
  13.6 0.2 select_reduce_fusion.2
  13.8 0.1 select_reduce_fusion.1
  13.9 0.3 dynamic-update-slice
  14.1 0.1 reshape.53
  14.3 0.2 copy.25
  14.5 57.0 %all-reduce.1 = s32[16,16,6]{0,1,2:T(8,128)S(1)} all-reduce(s32[16,16,6]{0,1,2:T(8,128)S(1)} %copy.25), channel_id=2, replica_groups=mesh['groups'=2,'cache_0'=8,'cache_1'=2,'tensor'=8] {'cache_0','cache_1'}, use_global_device_ids=true, to_apply=%add | all-reduce | flops 1536 | bytes 12288
  71.5 0.7 copy.33
  72.2 0.7 copy.34
  72.9 135.3 %ring_attention.1 = bf16[256,1024]{1,0:T(8,128)(2,1)} custom-call(s32[16,6]{1,0:T(8,128)} %bitcast.24, f32[16,6]{1,0:T(8,128)} %bitcast.25, bf16[256,1024]{1,0:T(8,128)(2,1)} %q_hbm.1, bf16[96,2,128,128]{3,2,1,0:T(8,128)(2,1)} %kv_hbm.1, bf16[2,256,128]{2,1,0:T(8,128)(2,1)} %suffix_hbm.1), custom_call_target="tpu_custom_call" | custom-call | flops 103079215104 | bytes 6291456 | tf_op jit(solution)/shard_map/ring_attention/pallas_call | solution.py:317
  208.2 0.0 all-gather.6.cloned.1.call-done
  208.2 0.0 copy-start
  208.2 7.1 %convert_bitcast_fusion.1 = bf16[16,256,256]{1,2,0:T(8,128)(2,1)S(1)} fusion(bf16[16,1024,256]{2,1,0:T(8,128)(2,1)} %bitcast.27, bf16[256,1024]{1,0:T(8,128)(2,1)} %ring_attention.1), kind=kOutput, calls=%fused_computation.2 | convolution fusion | flops 2148532224 | bytes 11010048 | tf_op jit(solution)/shard_map/vmap()/dot_general | solution.py:393
  215.3 0.0 all-gather.8.cloned.1.call-done
  215.3 0.0 copy-done
  215.3 6.8 %convert_bitcast_fusion = bf16[16,256,256]{1,2,0:T(8,128)(2,1)S(1)} fusion(bf16[16,1024,256]{2,1,0:T(8,128)(2,1)} %bitcast.28, bf16[256,1024]{1,0:T(8,128)(2,1)S(1)} %copy-done), kind=kOutput, calls=%fused_computation.1 | convolution fusion | flops 2148532224 | bytes 11010048 | tf_op jit(solution)/shard_map/vmap()/dot_general | solution.py:393
  222.1 2.3 pad_maximum_fusion
  224.4 6.4 %copy.30 = bf16[256,8192]{1,0:T(8,128)(2,1)} copy(bf16[256,8192]{0,1:T(8,128)(2,1)} %bitcast.23) | data formatting | bytes 8388608 | tf_op jit(solution)/shard_map/convert_element_type | solution.py:397
  230.8 0.1 reduce-scatter.2.cloned.1.call-update
  230.8 65.6 %reduce-scatter.2.cloned.1.call-done = bf16[256,1024]{1,0:T(8,128)(2,1)} async-done(((bf16[256,8192]{1,0:T(8,128)(2,1)}), bf16[256,1024]{1,0:T(8,128)(2,1)}) %reduce-scatter.2.cloned.1.call-update) | async-done | bytes 524304 | tf_op jit(solution)/shard_map/reduce_scatter | solution.py:396
  (6 shorter events, 0.1 us)
Async XLA Ops:
  6.5 201.6 %all-gather.6.cloned.1.call-start = ((), (), s32[]{:S(2)}) async-start(), calls=%async_computation.2 | async-start | bytes 8912896 | tf_op jit(solution)/shard_map/all_gather | solution.py:43
  8.8 206.4 %all-gather.8.cloned.1.call-start = ((), (), s32[]{:S(2)}) async-start(), calls=%async_computation.3 | async-start | bytes 8912896 | tf_op jit(solution)/shard_map/all_gather | solution.py:43
  9.7 286.8 %reduce-scatter.2.cloned.1.call-start = ((), (), s32[]{:S(2)}) async-start(), calls=%async_computation.1 | async-start | bytes 4718592 | tf_op jit(solution)/shard_map/reduce_scatter | solution.py:396
  208.2 7.1 %copy-start = (bf16[256,1024]{1,0:T(8,128)(2,1)S(1)}, bf16[256,1024]{1,0:T(8,128)(2,1)}, u32[]{:S(2)}) copy-start(bf16[256,1024]{1,0:T(8,128)(2,1)} %ring_attention.1) | copy-start | bytes 1572868
Sparse Core Ops, SparseCore 0:
  9.2 73.9 all-gather.5
  85.0 78.2 all-gather.7
  231.0 65.4 reduce-scatter.1

commit v2 on v1

--- a/solution.py
+++ b/solution.py
@@ -27,34 +27,20 @@
 MESH = pl.DeviceIdType.MESH
 
 
-def joined_along(parts, dim):
-    lengths = list(parts.shape[1:])
-    lengths[dim] *= parts.shape[0]
-    return jnp.moveaxis(parts, 0, dim).reshape(lengths)
-
-
-def on_gathered_pieces(shard, axis, dim, apply, out_dim):
-    peers, width = (lax.axis_size(axis), shard.shape[dim])
-    count = 2 if width % 2 == 0 else 1
-    finished, length = ([], width // count)
-    for k in range(count):
-        piece = lax.slice_in_dim(shard, k * length, (k + 1) * length, axis=dim)
-        starts = jnp.arange(peers) * width + k * length
-        finished.append(jax.vmap(apply)(lax.all_gather(piece, axis), starts))
-    return joined_along(jnp.concatenate(finished, axis=out_dim + 1), out_dim)
-
-
-def attention_kernel(
+def prefill_kernel(
     capacity,
     chips,
-    table,
-    live,
+    spans,
+    own_table,
+    table_hbm,
     q_hbm,
     kv_hbm,
     suffix_hbm,
-    out,
+    weight_hbm,
+    out_hbm,
     pool,
     suffix,
+    weight,
     q_all,
     part,
     partner_part,
@@ -65,7 +51,16 @@
     weights,
     tops,
     sums,
+    tables,
+    tables_in,
+    mixed_all,
+    terms,
+    terms_in,
+    finished,
+    landed,
     local_sem,
+    table_send,
+    table_recv,
     q_send,
     q_recv,
     q_core_send,
@@ -74,27 +69,63 @@
     p_core_recv,
     p_send,
     p_recv,
+    m_send,
+    m_recv,
+    m_core_send,
+    m_core_recv,
+    t_send,
+    t_recv,
+    f_send,
+    f_recv,
 ):
     x = lax.axis_index("cache_0")
     core = lax.axis_index("cache_1")
+    y = lax.axis_index("tensor")
+    me = 2 * x + core
+    caches = 2 * chips
+    slabs = caches // spans
+    goal = me // slabs
+    at_goal = goal == y
     right = {"cache_0": lax.rem(x + 1, chips), "cache_1": core}
     left = {"cache_0": lax.rem(x + chips - 1, chips), "cache_1": core}
     partner = {"cache_0": x, "cache_1": 1 - core}
+    up = {"tensor": lax.rem(y + 1, spans)}
+    down = {"tensor": lax.rem(y + spans - 1, spans)}
     far = chips // 2
+    far_span = spans // 2
     toward = (right, left)
+    toward_span = (up, down)
+    peers = [(dx, dk) for dx in range(chips) for dk in (0, 1)]
+
+    def cache_peer(dx, dk):
+        return {"cache_0": lax.rem(x + dx, chips), "cache_1": core if dk == 0 else 1 - core}
+
+    def source_peer(dj, dv):
+        cache = y * slabs + lax.rem(me + dj, slabs)
+        return {"cache_0": cache // 2, "cache_1": lax.rem(cache, 2), "tensor": lax.rem(y + dv, spans)}
 
     fetch_q = pltpu.make_async_copy(q_hbm, q_all.at[0, 0], local_sem.at[0])
-    fetch_pool = pltpu.make_async_copy(kv_hbm, pool, local_sem.at[1])
-    fetch_suffix = pltpu.make_async_copy(suffix_hbm, suffix, local_sem.at[2])
+    fetch_table = pltpu.make_async_copy(table_hbm, tables_in.at[0], local_sem.at[1])
+    fetch_pool = pltpu.make_async_copy(kv_hbm, pool, local_sem.at[2])
+    fetch_suffix = pltpu.make_async_copy(suffix_hbm, suffix, local_sem.at[3])
+    fetch_weight = pltpu.make_async_copy(weight_hbm, weight, local_sem.at[4])
     fetch_q.start()
+    fetch_table.start()
     fetch_pool.start()
     fetch_suffix.start()
+    fetch_weight.start()
     barrier = pltpu.get_barrier_semaphore()
-    for peer in (right, left, partner):
+    for dx, dk in peers[1:]:
+        pl.semaphore_signal(barrier, inc=1, device_id=cache_peer(dx, dk), device_id_type=MESH)
+    for peer in toward_span:
         pl.semaphore_signal(barrier, inc=1, device_id=peer, device_id_type=MESH)
+    for dj in range(slabs):
+        for dv in range(spans):
+            pl.semaphore_signal(barrier, inc=1, device_id=source_peer(dj, dv), device_id_type=MESH)
     values_t[HEAD_SIZE:, :] = jnp.ones((VALUE_ROWS - HEAD_SIZE, values_t.shape[1]), jnp.bfloat16)
     fetch_q.wait()
-    pl.semaphore_wait(barrier, 3)
+    fetch_table.wait()
+    pl.semaphore_wait(barrier, caches - 1 + 2 + caches)
 
     def chunk(offset, kind, half):
         return q_all.at[offset % chips, kind, pl.ds(half * HALF, HALF), :]
@@ -130,6 +161,20 @@
             device_id_type=MESH,
         )
 
+    def table_copy(dx, dk):
+        place = 2 * ((-dx) % chips) + dk
+        return pltpu.make_async_remote_copy(
+            src_ref=tables_in.at[0],
+            dst_ref=tables_in.at[place],
+            send_sem=table_send.at[place],
+            recv_sem=table_recv.at[place],
+            device_id=cache_peer(dx, dk),
+            device_id_type=MESH,
+        )
+
+    def table_load(place):
+        return pltpu.make_async_copy(tables_in.at[place], tables.at[place], local_sem.at[5])
+
     def p_copy(direction, distance, half):
         sign = 1 if direction == 0 else -1
         return pltpu.make_async_remote_copy(
@@ -143,12 +188,16 @@
 
     def attend(offset, kind, own):
         where = offset % chips
-        request = 2 * lax.rem(x + where, chips) + (core if kind == 0 else 1 - core)
+        place = 2 * where + kind
         pages = capacity + (SUF // PAGE_TOKENS if own else 0)
         alive = []
         for j in range(capacity):
-            row = table[request, j]
-            alive.append(live[request, j])
+            if own:
+                entry = own_table[0, me * capacity + j]
+            else:
+                entry = tables[place, 0, me * capacity + j]
+            row = jnp.maximum(entry - 1, 0)
+            alive.append(jnp.minimum(entry, 1).astype(jnp.float32))
             keys[j * PAGE_TOKENS : (j + 1) * PAGE_TOKENS, :] = pool[row, 0]
             values_t[0:HEAD_SIZE, j * PAGE_TOKENS : (j + 1) * PAGE_TOKENS] = pool[row, 1].T
         if own:
@@ -222,10 +271,17 @@
         for direction in (0, 1):
             q_copy(direction, 1, half).start()
         q_core_copy(0, half).start()
+    for dx, dk in peers[1:]:
+        table_copy(dx, dk).start()
     fetch_pool.wait()
     fetch_suffix.wait()
     attend(0, 0, True)
-    pending = []
+    for dx, dk in peers[1:]:
+        table_copy(dx, dk).wait_recv()
+        place = 2 * ((-dx) % chips) + dk
+        load = table_load(place)
+        load.start()
+        load.wait()
 
     def arrived(step, direction, half):
         q_copy(direction, step, half).wait_recv()
@@ -277,6 +333,30 @@
                     others.append(ring_in.at[direction, distance, half])
                 merge(part.at[offset, 0, half], others)
                 p_copy(direction, distance, half).start()
+    def mixed_chunk(offset, kind, half):
+        return mixed_all.at[offset % chips, kind, pl.ds(half * HALF, HALF), :]
+
+    def m_copy(direction, step, half):
+        sign = -1 if direction == 0 else 1
+        return pltpu.make_async_remote_copy(
+            src_ref=mixed_chunk(sign * (step - 1), 0, half),
+            dst_ref=mixed_chunk(sign * step, 0, half),
+            send_sem=m_send.at[direction, step - 1, half],
+            recv_sem=m_recv.at[direction, step - 1, half],
+            device_id=toward[direction],
+            device_id_type=MESH,
+        )
+
+    def m_core_copy(offset, half):
+        return pltpu.make_async_remote_copy(
+            src_ref=mixed_chunk(offset, 0, half),
+            dst_ref=mixed_chunk(offset, 1, half),
+            send_sem=m_core_send.at[offset % chips, half],
+            recv_sem=m_core_recv.at[offset % chips, half],
+            device_id=partner,
+            device_id_type=MESH,
+        )
+
     p_core_copy(0).wait_recv()
     for half in halves:
         for direction in (0, 1):
@@ -290,7 +370,172 @@
         for h in range(GROUP_WIDTH):
             rows = slice(h * HEAD_SIZE, (h + 1) * HEAD_SIZE)
             acc = sum(r[rows, :].astype(jnp.float32) * f[h : h + 1] for r, f in zip(refs, factors))
-            out[half * HALF : (half + 1) * HALF, rows] = acc.T.astype(jnp.bfloat16)
+            mixed_all[0, 0, half * HALF : (half + 1) * HALF, rows] = acc.T.astype(jnp.bfloat16)
+        for direction in (0, 1):
+            if far > 1 or half == direction:
+                m_copy(direction, 1, half).start()
+        m_core_copy(0, half).start()
+    fetch_weight.wait()
+
+    def mixed_arrived(step, direction, half):
+        m_copy(direction, step, half).wait_recv()
+        if step + 1 < far or (step + 1 == far and half == direction):
+            m_copy(direction, step + 1, half).start()
+        m_core_copy(-step if direction == 0 else step, half).start()
+
+    def t_copy(batch, direction, distance, half):
+        index, first, count = batch
+        sign = 1 if direction == 0 else -1
+        return pltpu.make_async_remote_copy(
+            src_ref=terms.at[(sign * distance) % spans, half, pl.ds(first, count)],
+            dst_ref=terms_in.at[direction, distance - 1, half, pl.ds(first, count)],
+            send_sem=t_send.at[index, direction, distance - 1, half],
+            recv_sem=t_recv.at[index, direction, distance - 1, half],
+            device_id=toward_span[direction],
+            device_id_type=MESH,
+        )
+
+    block_rows = terms.shape[3]
+    half_columns = terms.shape[4]
+    place_rows = pl.ds(pl.multiple_of(y * block_rows, block_rows), block_rows)
+    place_columns = pl.ds(pl.multiple_of(lax.rem(me, slabs) * 2 * half_columns, 2 * half_columns), 2 * half_columns)
+
+    def f_copy(slot, offset, kind):
+        target = dict(cache_peer(offset % chips, kind), tensor=goal)
+        return pltpu.make_async_remote_copy(
+            src_ref=finished.at[slot],
+            dst_ref=landed.at[place_rows, place_columns],
+            send_sem=f_send.at[slot],
+            recv_sem=f_recv.at[y, lax.rem(me, slabs)],
+            device_id=target,
+            device_id_type=MESH,
+        )
+
+    def project(slot, offset, kind):
+        term = jnp.dot(mixed_all[offset % chips, kind], weight[...], preferred_element_type=jnp.float32)
+        low = term.astype(jnp.bfloat16)
+        for block in range(spans):
+            where = lax.rem(block - y + spans, spans)
+            for half in halves:
+                terms[where, half, slot] = low[
+                    block * block_rows : (block + 1) * block_rows,
+                    half * half_columns : (half + 1) * half_columns,
+                ]
+
+    def reduce_terms(batch, members):
+        index, first, count = batch
+        here = pl.ds(first, count)
+
+        def passed_on(direction, distance, half):
+            where = (distance if direction == 0 else -distance) % spans
+            if distance < far_span - 1 or half == direction:
+                t_copy(batch, direction, distance + 1, half).wait_recv()
+                terms[where, half, here] = (
+                    terms[where, half, here].astype(jnp.float32)
+                    + terms_in[direction, distance, half, here].astype(jnp.float32)
+                ).astype(jnp.bfloat16)
+            t_copy(batch, direction, distance, half).start()
+
+        def finish(half):
+            for direction in (0, 1):
+                if far_span > 1 or half == direction:
+                    t_copy(batch, direction, 1, half).wait_recv()
+            total = terms[0, half, here].astype(jnp.float32)
+            for direction in (0, 1):
+                if far_span > 1 or half == direction:
+                    total = total + terms_in[direction, 0, half, here].astype(jnp.float32)
+            finished[here, :, half * half_columns : (half + 1) * half_columns] = total.astype(jnp.bfloat16)
+
+        for direction in (0, 1):
+            t_copy(batch, direction, far_span, direction).start()
+        if far_span > 1:
+            for direction in (0, 1):
+                passed_on(direction, far_span - 1, 1 - direction)
+        yield
+        for distance in range(far_span - 1, 0, -1):
+            for direction in (0, 1):
+                passed_on(direction, distance, direction)
+            if distance > 1:
+                for direction in (0, 1):
+                    passed_on(direction, distance - 1, 1 - direction)
+            yield
+        for half in halves:
+            finish(half)
+        for slot, (offset, kind) in enumerate(members, first):
+            if offset == 0 and kind == 0:
+
+                @pl.when(at_goal)
+                def _():
+                    landed[place_rows, place_columns] = finished[slot]
+
+                @pl.when(jnp.logical_not(at_goal))
+                def _():
+                    f_copy(slot, offset, kind).start()
+
+            else:
+                f_copy(slot, offset, kind).start()
+
+    batches = [[(0, 0), (0, 1)]]
+    for step in range(1, far):
+        batches.append([(-step, 0), (step, 0), (-step, 1), (step, 1)])
+    batches.append([(far, 0), (far, 1)])
+    active = []
+
+    def launch(index):
+        first = sum(len(b) for b in batches[:index])
+        for slot, (offset, kind) in enumerate(batches[index], first):
+            if kind == 1:
+                for half in halves:
+                    m_core_copy(offset, half).wait_recv()
+            project(slot, offset, kind)
+        active.append(reduce_terms((index, first, len(batches[index])), batches[index]))
+        next(active[-1])
+
+    def advance():
+        for item in list(active):
+            try:
+                next(item)
+            except StopIteration:
+                active.remove(item)
+
+    for step in range(1, far):
+        for direction in (0, 1):
+            mixed_arrived(step, direction, 0)
+        advance()
+        launch(step - 1)
+        for direction in (0, 1):
+            mixed_arrived(step, direction, 1)
+        advance()
+    mixed_arrived(far, 0, 0)
+    mixed_arrived(far, 1, 1)
+    advance()
+    launch(far - 1)
+    advance()
+    launch(far)
+    while active:
+        advance()
+
+    for dj in range(slabs):
+        for dv in range(spans):
+
+            def take():
+                block = lax.rem(y + dv, spans)
+                slab = lax.rem(me + dj, slabs)
+                pltpu.make_async_remote_copy(
+                    src_ref=finished.at[0],
+                    dst_ref=landed.at[place_rows, place_columns],
+                    send_sem=f_send.at[0],
+                    recv_sem=f_recv.at[block, slab],
+                    device_id=partner,
+                    device_id_type=MESH,
+                ).wait_recv()
+
+            if dj == 0 and dv == 0:
+                pl.when(jnp.logical_not(at_goal))(take)
+            else:
+                take()
+    store = pltpu.make_async_copy(landed, out_hbm, local_sem.at[6])
+    store.start()
 
     for direction in (0, 1):
         for half in halves:
@@ -298,36 +543,58 @@
                 if step < far or half == direction:
                     q_copy(direction, step, half).wait_send()
                     p_copy(direction, step, half).wait_send()
+                    m_copy(direction, step, half).wait_send()
+            for step in range(1, far_span + 1):
+                if step < far_span or half == direction:
+                    first = 0
+                    for index, members in enumerate(batches):
+                        t_copy((index, first, len(members)), direction, step, half).wait_send()
+                        first += len(members)
     for offset in range(chips):
         for half in halves:
             q_core_copy(offset, half).wait_send()
+            m_core_copy(offset, half).wait_send()
         p_core_copy(offset).wait_send()
-
-
-def attention(table, live, queries, kv_pages, suffix_key_value):
+    for dx, dk in peers[1:]:
+        table_copy(dx, dk).wait_send()
+    slot = 0
+    for members in batches:
+        for offset, kind in members:
+            if slot == 0:
+
+                @pl.when(jnp.logical_not(at_goal))
+                def _():
+                    f_copy(0, 0, 0).wait_send()
+
+            else:
+                f_copy(slot, offset, kind).wait_send()
+            slot += 1
+    store.wait()
+
+
+def prefill(table, queries, kv_pages, suffix_key_value, out_weight):
     chips = lax.axis_size("cache_0")
-    capacity = table.shape[1]
+    spans = lax.axis_size("tensor")
+    caches = 2 * chips
+    capacity = (3 * MAXP + 2 * caches - 1) // (2 * caches)
     far = chips // 2
+    far_span = spans // 2
     long = capacity * PAGE_TOKENS + SUF
+    width = out_weight.shape[1]
     bf16 = jnp.bfloat16
-    requests = table.shape[0]
     any_space = pl.BlockSpec(memory_space=pl.ANY)
-    flops = 4 * requests * GROUP_WIDTH * SUF * HEAD_SIZE * capacity * PAGE_TOKENS
+    flops = 4 * caches * GROUP_WIDTH * SUF * HEAD_SIZE * capacity * PAGE_TOKENS
     dma = pltpu.SemaphoreType.DMA
+    out_shape = (SUF, width * caches // spans)
     return pl.pallas_call(
-        functools.partial(attention_kernel, capacity, chips),
-        out_shape=jax.ShapeDtypeStruct(queries.shape, bf16),
-        in_specs=[
-            pl.BlockSpec(memory_space=pltpu.SMEM),
-            pl.BlockSpec(memory_space=pltpu.SMEM),
-            any_space,
-            any_space,
-            any_space,
-        ],
-        out_specs=pl.BlockSpec(memory_space=pltpu.VMEM),
+        functools.partial(prefill_kernel, capacity, chips, spans),
+        out_shape=jax.ShapeDtypeStruct(out_shape, bf16),
+        in_specs=[pl.BlockSpec(memory_space=pltpu.SMEM)] + [any_space] * 5,
+        out_specs=any_space,
         scratch_shapes=[
             pltpu.VMEM(kv_pages.shape, bf16),
             pltpu.VMEM(suffix_key_value.shape, bf16),
+            pltpu.VMEM(out_weight.shape, bf16),
             pltpu.VMEM((chips, 2) + queries.shape, bf16),
             pltpu.VMEM((chips, 2, 2, PART_ROWS, HALF), bf16),
             pltpu.VMEM((chips, 2, PART_ROWS, HALF), bf16),
@@ -338,7 +605,16 @@
             pltpu.VMEM((long, SUF), bf16),
             pltpu.VMEM((GROUP_WIDTH, SUF), jnp.float32),
             pltpu.VMEM((GROUP_WIDTH, SUF), jnp.float32),
-            dma((3,)),
+            pltpu.SMEM((caches,) + table.shape, jnp.int32),
+            pltpu.VMEM((caches,) + table.shape, jnp.int32),
+            pltpu.VMEM((chips, 2) + queries.shape, bf16),
+            pltpu.VMEM((spans, 2, caches, SUF // spans, width // 2), bf16),
+            pltpu.VMEM((2, far_span, 2, caches, SUF // spans, width // 2), bf16),
+            pltpu.VMEM((caches, SUF // spans, width), bf16),
+            pltpu.VMEM(out_shape, bf16),
+            dma((7,)),
+            dma((caches,)),
+            dma((caches,)),
             dma((2, far, 2)),
             dma((2, far, 2)),
             dma((chips, 2)),
@@ -347,15 +623,23 @@
             dma((chips,)),
             dma((2, far, 2)),
             dma((2, far, 2)),
+            dma((2, far, 2)),
+            dma((2, far, 2)),
+            dma((chips, 2)),
+            dma((chips, 2)),
+            dma((far + 1, 2, far_span, 2)),
+            dma((far + 1, 2, far_span, 2)),
+            dma((caches,)),
+            dma((spans, caches // spans)),
         ],
         compiler_params=pltpu.CompilerParams(
-            collective_id=0, has_side_effects=True, vmem_limit_bytes=60 * 1024 * 1024
+            collective_id=0, has_side_effects=True, vmem_limit_bytes=62 * 1024 * 1024
         ),
         cost_estimate=pl.CostEstimate(
-            flops=8 * flops, bytes_accessed=kv_pages.size * 2, transcendentals=0
+            flops=flops, bytes_accessed=kv_pages.size * 2, transcendentals=0
         ),
-        name="ring_attention",
-    )(table, live, queries, kv_pages, suffix_key_value)
+        name="prefill",
+    )(table, table, queries, kv_pages, suffix_key_value, out_weight)
 
 
 def slot_tables(kv_pages, page_ids, prefix_pages, page_home):
@@ -380,23 +664,13 @@
     wanted = jnp.sum(
         jnp.where(target[:, None] == buffer_index[None, :], within[:, None] + 1, 0), axis=0
     )
-    everyone = lax.all_gather(wanted, CACHE).reshape(cache_count, cache_count, capacity)
-    mine = lax.dynamic_index_in_dim(everyone, lax.axis_index(CACHE), 1, keepdims=False)
-    return jnp.maximum(mine - 1, 0), (mine > 0).astype(jnp.float32)
+    lanes = 128 * ((wanted.shape[0] + 127) // 128)
+    return jnp.pad(wanted, (0, lanes - wanted.shape[0]))[None, :]
 
 
 def per_device(queries, suffix_key_value, kv_pages, page_ids, prefix_pages, page_home, out_weight):
-    table, live = slot_tables(kv_pages, page_ids, prefix_pages, page_home)
-    outputs = attention(table, live, queries, kv_pages, suffix_key_value)
-
-    def project(weight_piece, start_column):
-        return jnp.dot(outputs, weight_piece, preferred_element_type=jnp.float32)
-
-    group_term = on_gathered_pieces(out_weight, CACHE, 1, project, 1)
-    attended = lax.psum_scatter(
-        group_term.astype(jnp.bfloat16), "tensor", scatter_dimension=1, tiled=True
-    )
-    return attended
+    table = slot_tables(kv_pages, page_ids, prefix_pages, page_home)
+    return prefill(table, queries, kv_pages, suffix_key_value, out_weight)
 
 
 def solution(mesh):

time: 305 us -> 253 us (0.83)
  Pallas kernels: 135 us -> 247 us
  waiting for transfers between devices: 66.5 us -> 0 us
  blocking collectives: 57 us -> 0 us
  between operations: 14.6 us -> 0.69 us
  matrix products: 13.9 us -> 0 us
  local copies, waits for them, and re-layouts: 11.9 us -> 2.39 us
    pallas_call x1, Pallas kernels: 135 us -> 247 us  [prefill(): pl.pallas_call(functools.partial(prefill_kernel, capacity, chips, spans),...]
    reduce_scatter x1 -> x0, waiting for transfers between devices: 65.6 us -> none  [per_device(): lax.psum_scatter(group_term.astype(jnp.bfloat16), 'tensor', scatter_dimen...]
    unnamed x1 -> x0, blocking collectives: 57 us -> none
    dot_general x2 -> x0, matrix products: 13.9 us -> none  [project(): return jnp.dot(outputs, weight_piece, preferred_element_type=jnp.float32)]
    convert_element_type x2 -> x0, local copies, waits for them, and re-layouts: 7.05 us -> none  [the longest x1 6.38 us: per_device(): group_term.astype(jnp.bfloat16)]
  transfers between devices with their start and end apart: 3 -> 0, of which waited for: 1 -> 0; matrix products, arithmetic and copies ran while one was open for 4% -> 0% of each run, Pallas kernels for 45% -> 0%
where the time goes in v2:
time: 253 us; the launch traced here: 251 us
  Pallas kernels  247 us (98%)
    pallas_call x1, Pallas kernels, prefill(): pl.pallas_call(functools.partial(prefill_kernel, capacity, chips, spans),...  247 us

profile of v2, /device:TPU:521, one launch (start us, length us, event | category | flops | bytes accessed | tf_op | source)
XLA Modules:
  0.0 251.5 jit_solution(5350245842965413048)
XLA Ops:
  0.7 0.9 select_reduce_fusion
  1.6 0.1 fusion.1
  1.7 0.1 reduce_window_sum.11
  1.8 0.2 select_reduce_fusion.2
  2.0 0.1 select_reduce_fusion.1
  2.1 0.5 pad_bitcast_fusion.own_table.table_hbm
  2.6 247.0 %prefill.1 = bf16[256,1024]{1,0:T(8,128)(2,1)} custom-call(s32[1,128]{1,0:T(1,128)} %pad_bitcast_fusion.own_table.table_hbm, s32[1,128]{1,0:T(1,128)} %pad_bitcast_fusion.own_table.table_hbm, bf16[256,1024]{1,0:T(8,128)(2,1)} %q_hbm.1, bf16[96,2,128,128]{3,2,1,0:T(8,128)(2,1)} %kv_hbm.1, bf16[2,256,128]{2,1,0:T(8,128)(2,1)} %suffix_hbm.1, ...), custom_call_target="tpu_custom_call" | custom-call | flops 12884901888 | bytes 6291456 | tf_op jit(solution)/shard_map/prefill/pallas_call | solution.py:589
  249.6 1.9 copy.10
  (3 shorter events, 0.0 us)

commit v3 on v2

--- a/solution.py
+++ b/solution.py
@@ -204,7 +204,9 @@
             keys[capacity * PAGE_TOKENS :, :] = suffix[0]
             values_t[0:HEAD_SIZE, capacity * PAGE_TOKENS :] = suffix[1].T
 
-        def head(h, carry):
+        length = pages * PAGE_TOKENS
+
+        def score(h, slot):
             q_head = q_all[where, kind, :, pl.ds(pl.multiple_of(h * HEAD_SIZE, HEAD_SIZE), HEAD_SIZE)]
             top = None
             for j in range(pages):
@@ -216,29 +218,36 @@
                     key_at = lax.broadcasted_iota(jnp.int32, piece.shape, 0) + (j - capacity) * PAGE_TOKENS
                     token_at = lax.broadcasted_iota(jnp.int32, piece.shape, 1)
                     piece = jnp.where(key_at <= token_at, piece, -DEAD)
-                scores[span, :] = piece
+                scores[slot, span, :] = piece
                 peak = jnp.max(piece, axis=0, keepdims=True)
                 if j < capacity:
                     peak = peak * alive[j] + (alive[j] - 1.0) * DEAD
                 top = peak if top is None else jnp.maximum(top, peak)
-            level = jnp.ceil(top * (LOG2_SCALE * 0.25)) * 4.0
+            return jnp.ceil(top * (LOG2_SCALE * 0.25)) * 4.0
+
+        def gather_values(h, slot, level):
             for j in range(pages):
                 span = pl.ds(j * PAGE_TOKENS, PAGE_TOKENS)
                 shift = -level
                 if j < capacity:
                     shift = shift * alive[j] + (alive[j] - 1.0) * DEAD
-                weights[span, :] = jnp.exp2(scores[span, :] * LOG2_SCALE + shift).astype(jnp.bfloat16)
-            length = pages * PAGE_TOKENS
-            mixed = jnp.dot(values_t[:, 0:length], weights[0:length, :], preferred_element_type=jnp.float32)
+                weights[slot, span, :] = jnp.exp2(scores[slot, span, :] * LOG2_SCALE + shift).astype(jnp.bfloat16)
+            mixed = jnp.dot(values_t[:, 0:length], weights[slot, 0:length, :], preferred_element_type=jnp.float32)
             rows = pl.ds(pl.multiple_of(h * HEAD_SIZE, HEAD_SIZE), HEAD_SIZE)
             low = mixed[0:HEAD_SIZE].astype(jnp.bfloat16)
             part[where, kind, 0, rows, :] = low[:, 0:HALF]
             part[where, kind, 1, rows, :] = low[:, HALF:]
             tops[pl.ds(h, 1), :] = level
             sums[pl.ds(h, 1), :] = mixed[HEAD_SIZE : HEAD_SIZE + 1]
-            return carry
-
-        lax.fori_loop(0, GROUP_WIDTH, head, 0)
+
+        def two_heads(i, level):
+            later = score(2 * i + 1, 1)
+            gather_values(2 * i, 0, level)
+            following = score(jnp.minimum(2 * i + 2, GROUP_WIDTH - 1), 0)
+            gather_values(2 * i + 1, 1, later)
+            return following
+
+        lax.fori_loop(0, GROUP_WIDTH // 2, two_heads, score(0, 0))
         for half in range(2):
             lanes = pl.ds(half * HALF, HALF)
             put_stats(part.at[where, kind, half], tops[:, lanes], sums[:, lanes])
@@ -295,30 +304,33 @@
         attend(offset, 1, False)
         p_core_copy(offset).start()
 
+    other_core(0)
+    for direction in (0, 1):
+        arrived(1, direction, 0)
     for step in range(1, far):
-        for direction in (0, 1):
-            arrived(step, direction, 0)
-        if step == 1:
-            other_core(0)
-        else:
-            other_core(1 - step)
-            other_core(step - 1)
         for direction in (0, 1):
             arrived(step, direction, 1)
         attend(-step, 0, False)
         attend(step, 0, False)
+        if step + 1 < far:
+            other_core(-step)
+            for direction in (0, 1):
+                arrived(step + 1, direction, 0)
+            other_core(step)
+    if far > 1:
+        other_core(1 - far)
     arrived(far, 0, 0)
     arrived(far, 1, 1)
     attend(far, 0, False)
     other_core(far)
-    other_core(1 - far)
-    other_core(far - 1)
 
     p_core_copy(far).wait_recv()
     for direction in (0, 1):
         half = direction
         merge(part.at[far, 0, half], [partner_part.at[far, half]])
         p_copy(direction, far, half).start()
+    if far > 1:
+        other_core(far - 1)
     for distance in range(far - 1, 0, -1):
         for direction in (0, 1):
             offset = (distance if direction == 0 else -distance) % chips
@@ -498,18 +510,17 @@
             except StopIteration:
                 active.remove(item)
 
+    launch(0)
     for step in range(1, far):
         for direction in (0, 1):
             mixed_arrived(step, direction, 0)
         advance()
-        launch(step - 1)
         for direction in (0, 1):
             mixed_arrived(step, direction, 1)
         advance()
+        launch(step)
     mixed_arrived(far, 0, 0)
     mixed_arrived(far, 1, 1)
-    advance()
-    launch(far - 1)
     advance()
     launch(far)
     while active:
@@ -601,8 +612,8 @@
             pltpu.VMEM((2, far, 2, PART_ROWS, HALF), bf16),
             pltpu.VMEM((long, HEAD_SIZE), bf16),
             pltpu.VMEM((VALUE_ROWS, long), bf16),
-            pltpu.VMEM((long, SUF), jnp.float32),
-            pltpu.VMEM((long, SUF), bf16),
+            pltpu.VMEM((2, long, SUF), jnp.float32),
+            pltpu.VMEM((2, long, SUF), bf16),
             pltpu.VMEM((GROUP_WIDTH, SUF), jnp.float32),
             pltpu.VMEM((GROUP_WIDTH, SUF), jnp.float32),
             pltpu.SMEM((caches,) + table.shape, jnp.int32),

time: 253 us -> 228 us (0.901)
  Pallas kernels: 247 us -> 224 us
    pallas_call x1, Pallas kernels: 247 us -> 224 us  [prefill(): pl.pallas_call(functools.partial(prefill_kernel, capacity, chips, spans),...]
where the time goes in v3:
time: 228 us
  Pallas kernels  224 us (98%)
  local copies, waits for them, and re-layouts  2.39 us (1%)
    pallas_call x1, Pallas kernels, prefill(): pl.pallas_call(functools.partial(prefill_kernel, capacity, chips, spans),...  224 us

profile of v3, /device:TPU:521, one launch (start us, length us, event | category | flops | bytes accessed | tf_op | source)
XLA Modules:
  0.0 228.0 jit_solution(12140054087524222785)
XLA Ops:
  0.7 0.9 select_reduce_fusion
  1.6 0.1 fusion.1
  1.7 0.1 reduce_window_sum.11
  1.8 0.2 select_reduce_fusion.2
  2.0 0.1 select_reduce_fusion.1
  2.1 0.5 pad_bitcast_fusion.own_table.table_hbm
  2.6 223.5 %prefill.1 = bf16[256,1024]{1,0:T(8,128)(2,1)} custom-call(s32[1,128]{1,0:T(1,128)} %pad_bitcast_fusion.own_table.table_hbm, s32[1,128]{1,0:T(1,128)} %pad_bitcast_fusion.own_table.table_hbm, bf16[256,1024]{1,0:T(8,128)(2,1)} %q_hbm.1, bf16[96,2,128,128]{3,2,1,0:T(8,128)(2,1)} %kv_hbm.1, bf16[2,256,128]{2,1,0:T(8,128)(2,1)} %suffix_hbm.1, ...), custom_call_target="tpu_custom_call" | custom-call | flops 12884901888 | bytes 6291456 | tf_op jit(solution)/shard_map/prefill/pallas_call | solution.py:600
  226.2 1.9 copy.10
  (3 shorter events, 0.0 us)

commit v4 on v3

--- a/solution.py
+++ b/solution.py
@@ -172,8 +172,7 @@
             device_id_type=MESH,
         )
 
-    def table_load(place):
-        return pltpu.make_async_copy(tables_in.at[place], tables.at[place], local_sem.at[5])
+    table_load = pltpu.make_async_copy(tables_in, tables, local_sem.at[5])
 
     def p_copy(direction, distance, half):
         sign = 1 if direction == 0 else -1
@@ -287,10 +286,8 @@
     attend(0, 0, True)
     for dx, dk in peers[1:]:
         table_copy(dx, dk).wait_recv()
-        place = 2 * ((-dx) % chips) + dk
-        load = table_load(place)
-        load.start()
-        load.wait()
+    table_load.start()
+    table_load.wait()
 
     def arrived(step, direction, half):
         q_copy(direction, step, half).wait_recv()
@@ -319,32 +316,41 @@
             other_core(step)
     if far > 1:
         other_core(1 - far)
-    arrived(far, 0, 0)
-    arrived(far, 1, 1)
+        arrived(far, 0, 0)
+        arrived(far, 1, 1)
+        other_core(far - 1)
+    else:
+        arrived(far, 0, 0)
+        arrived(far, 1, 1)
     attend(far, 0, False)
+
+    def pass_on(direction, distance, half):
+        offset = (distance if direction == 0 else -distance) % chips
+        others = [partner_part.at[offset, half]]
+        if distance < far - 1 or (distance == far - 1 and half == direction):
+            p_copy(direction, distance + 1, half).wait_recv()
+            others.append(ring_in.at[direction, distance, half])
+        merge(part.at[offset, 0, half], others)
+        p_copy(direction, distance, half).start()
+
+    if far > 1:
+        for direction in (0, 1):
+            p_core_copy(far - 1 if direction == 0 else 1 - far).wait_recv()
+        for direction in (0, 1):
+            pass_on(direction, far - 1, 1 - direction)
     other_core(far)
-
     p_core_copy(far).wait_recv()
     for direction in (0, 1):
-        half = direction
-        merge(part.at[far, 0, half], [partner_part.at[far, half]])
-        p_copy(direction, far, half).start()
-    if far > 1:
-        other_core(far - 1)
+        pass_on(direction, far, direction)
     for distance in range(far - 1, 0, -1):
-        for direction in (0, 1):
-            offset = (distance if direction == 0 else -distance) % chips
-            p_core_copy(offset).wait_recv()
-        for turn in (0, 1):
+        if distance < far - 1:
             for direction in (0, 1):
-                offset = (distance if direction == 0 else -distance) % chips
-                half = direction if turn == 1 else 1 - direction
-                others = [partner_part.at[offset, half]]
-                if distance < far - 1 or half == direction:
-                    p_copy(direction, distance + 1, half).wait_recv()
-                    others.append(ring_in.at[direction, distance, half])
-                merge(part.at[offset, 0, half], others)
-                p_copy(direction, distance, half).start()
+                p_core_copy(distance if direction == 0 else -distance).wait_recv()
+            for direction in (0, 1):
+                pass_on(direction, distance, 1 - direction)
+        for direction in (0, 1):
+            pass_on(direction, distance, direction)
+
     def mixed_chunk(offset, kind, half):
         return mixed_all.at[offset % chips, kind, pl.ds(half * HALF, HALF), :]
 
@@ -371,9 +377,14 @@
 
     p_core_copy(0).wait_recv()
     for half in halves:
-        for direction in (0, 1):
-            p_copy(direction, 1, half).wait_recv()
-        refs = [part.at[0, 0, half], partner_part.at[0, half], ring_in.at[0, 0, half], ring_in.at[1, 0, half]]
+        others = [partner_part.at[0, half]]
+        if far > 1:
+            p_copy(1 - half, 1, half).wait_recv()
+            others.append(ring_in.at[1 - half, 0, half])
+        merge(part.at[0, 0, half], others)
+    for half in halves:
+        p_copy(half, 1, half).wait_recv()
+        refs = [part.at[0, 0, half], ring_in.at[half, 0, half]]
         pairs = [get_stats(r) for r in refs]
         top = functools.reduce(jnp.maximum, [p[0] for p in pairs])
         factors = [jnp.exp2(p[0] - top) for p in pairs]

time: 228 us -> 222 us (0.974)
  Pallas kernels: 224 us -> 217 us
    pallas_call x1, Pallas kernels: 224 us -> 217 us  [prefill(): pl.pallas_call(functools.partial(prefill_kernel, capacity, chips, spans),...]
where the time goes in v4:
time: 222 us
  Pallas kernels  217 us (98%)
  local copies, waits for them, and re-layouts  2.39 us (1%)
    pallas_call x1, Pallas kernels, prefill(): pl.pallas_call(functools.partial(prefill_kernel, capacity, chips, spans),...  217 us

profile of v4, /device:TPU:521, one launch (start us, length us, event | category | flops | bytes accessed | tf_op | source)
XLA Modules:
  0.0 222.0 jit_solution(17042692660147685584)
XLA Ops:
  0.7 0.9 select_reduce_fusion
  1.6 0.1 fusion.1
  1.7 0.1 reduce_window_sum.11
  1.8 0.2 select_reduce_fusion.2
  2.0 0.1 select_reduce_fusion.1
  2.1 0.5 pad_bitcast_fusion.own_table.table_hbm
  2.6 217.5 %prefill.1 = bf16[256,1024]{1,0:T(8,128)(2,1)} custom-call(s32[1,128]{1,0:T(1,128)} %pad_bitcast_fusion.own_table.table_hbm, s32[1,128]{1,0:T(1,128)} %pad_bitcast_fusion.own_table.table_hbm, bf16[256,1024]{1,0:T(8,128)(2,1)} %q_hbm.1, bf16[96,2,128,128]{3,2,1,0:T(8,128)(2,1)} %kv_hbm.1, bf16[2,256,128]{2,1,0:T(8,128)(2,1)} %suffix_hbm.1, ...), custom_call_target="tpu_custom_call" | custom-call | flops 12884901888 | bytes 6291456 | tf_op jit(solution)/shard_map/prefill/pallas_call | solution.py:611
  220.1 1.9 copy.10
  (3 shorter events, 0.0 us)

commit v5 on v4

--- a/solution.py
+++ b/solution.py
@@ -514,8 +514,8 @@
         active.append(reduce_terms((index, first, len(batches[index])), batches[index]))
         next(active[-1])
 
-    def advance():
-        for item in list(active):
+    def advance(newest_first=False):
+        for item in active[::-1] if newest_first else list(active):
             try:
                 next(item)
             except StopIteration:
@@ -532,10 +532,9 @@
         launch(step)
     mixed_arrived(far, 0, 0)
     mixed_arrived(far, 1, 1)
-    advance()
     launch(far)
     while active:
-        advance()
+        advance(newest_first=True)
 
     for dj in range(slabs):
         for dv in range(spans):

time: 222 us -> 220 us (level); the launches traced: 222 us -> 217 us
  Pallas kernels: 217 us -> 213 us
    pallas_call x1, Pallas kernels: 217 us -> 213 us  [prefill(): pl.pallas_call(functools.partial(prefill_kernel, capacity, chips, spans),...]
where the time goes in v5:
time: 220 us; the launch traced here: 217 us
  Pallas kernels  213 us (97%)
  local copies, waits for them, and re-layouts  2.39 us (1%)
    pallas_call x1, Pallas kernels, prefill(): pl.pallas_call(functools.partial(prefill_kernel, capacity, chips, spans),...  213 us

profile of v5, /device:TPU:521, one launch (start us, length us, event | category | flops | bytes accessed | tf_op | source)
XLA Modules:
  0.0 217.1 jit_solution(18239557228653010023)
XLA Ops:
  0.7 0.9 select_reduce_fusion
  1.6 0.1 fusion.1
  1.7 0.1 reduce_window_sum.11
  1.8 0.2 select_reduce_fusion.2
  2.0 0.1 select_reduce_fusion.1
  2.1 0.5 pad_bitcast_fusion.own_table.table_hbm
  2.6 212.6 %prefill.1 = bf16[256,1024]{1,0:T(8,128)(2,1)} custom-call(s32[1,128]{1,0:T(1,128)} %pad_bitcast_fusion.own_table.table_hbm, s32[1,128]{1,0:T(1,128)} %pad_bitcast_fusion.own_table.table_hbm, bf16[256,1024]{1,0:T(8,128)(2,1)} %q_hbm.1, bf16[96,2,128,128]{3,2,1,0:T(8,128)(2,1)} %kv_hbm.1, bf16[2,256,128]{2,1,0:T(8,128)(2,1)} %suffix_hbm.1, ...), custom_call_target="tpu_custom_call" | custom-call | flops 12884901888 | bytes 6291456 | tf_op jit(solution)/shard_map/prefill/pallas_call | solution.py:610
  215.2 1.9 copy.10
  (3 shorter events, 0.0 us)
